TPU v7x, 256 devices: a whole 4x4x8 slice. The times are simulated.
256 devices in a mesh: fsdp: 32 (over z, y), tp: 4 (over x), job: 2 (over core).
Axes of the slice: x: 4, y: 4, z: 8, core: 2. Of those that a mesh axis runs over, the one named last changes fastest.
Arguments:
- slopes_in: float32 [1024, 128, 1024], P('job', 'fsdp', 'tp'), parts along dimension 0, may hold values from -6 to 6
- moments_in: float32 [1024, 128, 1024], P('job', 'fsdp', 'tp'), parts along dimension 0, may hold values from -6 to 6
- weights_in: float32 [1024, 128, 1024], P('job', 'fsdp', 'tp'), parts along dimension 0, may hold values from -0.1875 to 0.1875
Outputs:
- new_weights: float32 [1024, 128, 1024], P('job', 'fsdp', 'tp'), parts along dimension 0
- new_momentum: float32 [1024, 128, 1024], P('job', 'fsdp', 'tp'), parts along dimension 0
There are 2 independent parts, one for each index of `job`. A program takes and returns all parts, laid end to end along the dimension named above; each array names one. Nothing has to cross between parts.
All inputs are finite; a program needn't handle non-finite values.
Results may differ from a plain program's by a relative error of at most 0.00019.
Values sent between devices are 32-bit elements; how exact they have to be, the bound alone decides.
No kernel may reach another device: no remote copies, remote signals or barrier semaphores. Data moves between devices by JAX's collectives and lax.ppermute only.
A program may use at most 128 MiB of HBM per device.

v0:
```python
import jax
import jax.numpy as jnp
from jax import lax
from jax.sharding import PartitionSpec as P

ITERS = 5


hold_rate = 0.9
learn_rate = 0.8


def split_up(value, dim, devices):
    lengths = value.shape
    pieces = value.reshape(*lengths[:dim], devices, lengths[dim] // devices, *lengths[dim + 1 :])
    return jnp.moveaxis(pieces, dim, 0)


def edges_of(length, count):
    unit = 8 if length >= 8 * count else 1
    return [length // unit * k // count * unit for k in range(1, count)]


def laid_out(pieces, dim):
    lengths = list(pieces.shape[1:])
    lengths[dim] *= pieces.shape[0]
    return jnp.moveaxis(pieces, 0, dim).reshape(lengths)


def cut_exchange(value, axis, pieces, split_dim, concat_dim):
    blocks = split_up(value, split_dim, lax.axis_size(axis))
    split_at = max(range(1, max(2, blocks.ndim - 1)), key=lambda d: blocks.shape[d])
    finished = []
    for share in jnp.split(blocks, edges_of(blocks.shape[split_at], pieces), axis=split_at):
        if share.size:
            finished.append(lax.all_to_all(share, axis, split_axis=0, concat_axis=0, tiled=True))
    return laid_out(jnp.concatenate(finished, axis=split_at), concat_dim)


def body(slopes_in, moments_in, weights_in):
    new_momentum = hold_rate * moments_in + slopes_in
    moved = lax.all_to_all(new_momentum, "fsdp", split_axis=0, concat_axis=1, tiled=True)
    whole = lax.all_to_all(moved, "tp", split_axis=0, concat_axis=2, tiled=True)
    iterate = whole * lax.rsqrt(jnp.sum(whole * whole, axis=(1, 2), keepdims=True) + 1e-06)
    for step in range(ITERS):
        gram = jnp.einsum("mik,mjk->mij", iterate, iterate, precision=lax.Precision.HIGHEST)
        mixed = -4.775 * gram + 2.0315 * jnp.einsum(
            "mij,mjk->mik", gram, gram, precision=lax.Precision.HIGHEST
        )
        iterate = 3.4445 * iterate + jnp.einsum(
            "mij,mjk->mik", mixed, iterate, precision=lax.Precision.HIGHEST
        )
    iterate = cut_exchange(iterate, "tp", 2, 2, 0)
    back = lax.all_to_all(iterate, "fsdp", split_axis=1, concat_axis=0, tiled=True)
    new_weights = weights_in - learn_rate * back
    return (new_weights, new_momentum)


def solution(mesh):
    placed = (P("job", "fsdp", "tp"), P("job", "fsdp", "tp"), P("job", "fsdp", "tp"))
    return jax.shard_map(
        body,
        mesh=mesh,
        in_specs=placed,
        out_specs=(P("job", "fsdp", "tp"), P("job", "fsdp", "tp")),
        check_vma=False,
    )
```

profile of v0, /device:TPU:16, one launch (start us, length us, event | category | flops | bytes accessed | tf_op | source)
XLA Modules:
  0.0 210.5 jit_solution(15059887878700993549)
XLA Ops:
  0.6 2.9 %multiply_add_fusion.5 = f32[512,4,256]{2,1,0:T(4,128)S(1)} fusion(f32[512,4,256]{2,1,0:T(4,128)} %param.3, f32[512,4,256]{2,1,0:T(4,128)} %param.4), kind=kLoop, calls=%fused_computation.9 | loop fusion | flops 1048576 | bytes 6291456 | tf_op jit(solution)/shard_map/add | solution.py:41
  3.6 61.9 %all_to_all.55 = f32[512,4,256]{2,1,0:T(4,128)S(1)} all-to-all(f32[512,4,256]{2,1,0:T(4,128)S(1)} %multiply_add_fusion.5), channel_id=1, replica_groups=mesh['fsdp'=32,'tp'=4,'job'=2] {'fsdp'}, dimensions={0} | all-to-all | bytes 4194304 | tf_op jit(solution)/shard_map/all_to_all | solution.py:42
  65.5 0.4 copy.20
  65.9 0.2 copy.21
  66.2 1.2 copy.22
  67.4 29.0 %all_to_all.56 = f32[16,128,256]{2,1,0:T(8,128)S(1)} all-to-all(f32[16,128,256]{2,1,0:T(8,128)S(1)} %copy.22), channel_id=1, replica_groups=mesh['fsdp'=32,'tp'=4,'job'=2] {'tp'}, dimensions={0} | all-to-all | bytes 4194304 | tf_op jit(solution)/shard_map/all_to_all | solution.py:43
  96.4 0.3 multiply_reduce_fusion
  96.7 0.2 copy.30
  96.9 2.3 %fusion.2 = f32[4,128,128]{2,1,0:T(8,128)S(1)} fusion(f32[4,128,1024]{2,1,0:T(8,128)S(1)} %bitcast.49, f32[4]{0:T(128)S(1)} %add_rsqrt_fusion), kind=kOutput, calls=%fused_computation.12 | convolution fusion | flops 805830656 | bytes 2359312 | tf_op jit(solution)/shard_map/mik,mjk->mij/dot_general | solution.py:46
  99.2 0.4 fusion.10
  99.6 2.1 %multiply_add_fusion.4 = f32[4,128,1024]{2,1,0:T(8,128)S(1)} fusion(f32[4,128,1024]{2,1,0:T(8,128)S(1)} %bitcast.50, f32[4,128,128]{2,1,0:T(8,128)S(1)} %fusion.10, f32[4]{0:T(128)S(1)} %add_rsqrt_fusion), kind=kOutput, calls=%fused_computation.7 | convolution fusion | flops 807403520 | bytes 4456464 | tf_op jit(solution)/shard_map/mij,mjk->mik/dot_general | solution.py:50
  101.7 2.0 fusion.14
  103.8 0.4 fusion.9
  104.1 2.1 multiply_add_fusion.3
  106.2 2.0 fusion.15
  108.3 0.4 fusion.8
  108.7 2.3 %multiply_add_fusion.2 = f32[4,128,1024]{2,1,0:T(8,128)S(1)} fusion(f32[4,128,1024]{2,1,0:T(8,128)S(1)} %multiply_add_fusion.3, f32[4,128,128]{2,1,0:T(8,128)S(1)} %fusion.8), kind=kOutput, calls=%fused_computation.5 | convolution fusion | flops 806354944 | bytes 4456448 | tf_op jit(solution)/shard_map/mij,mjk->mik/dot_general | solution.py:50
  111.0 2.0 fusion.16
  113.0 0.4 fusion.7
  113.4 2.1 multiply_add_fusion.1
  115.5 2.1 fusion.17
  117.6 0.4 fusion.6
  117.9 2.1 multiply_add_fusion
  120.4 15.2 %all_to_all.57 = f32[4,4,64,256]{3,2,1,0:T(8,128)S(1)} all-to-all(f32[4,4,64,256]{3,2,1,0:T(8,128)S(1)} %get-tuple-element.6), channel_id=1, replica_groups=mesh['fsdp'=32,'tp'=4,'job'=2] {'tp'}, dimensions={0} | all-to-all | bytes 2097152 | tf_op jit(solution)/shard_map/all_to_all | solution.py:36
  135.6 14.3 %all_to_all.58 = f32[4,4,64,256]{3,2,1,0:T(8,128)S(1)} all-to-all(f32[4,4,64,256]{3,2,1,0:T(8,128)S(1)} %get-tuple-element.7), channel_id=1, replica_groups=mesh['fsdp'=32,'tp'=4,'job'=2] {'tp'}, dimensions={0} | all-to-all | bytes 2097152 | tf_op jit(solution)/shard_map/all_to_all | solution.py:36
  150.1 1.2 copy.25
  151.3 54.2 %all_to_all.59 = f32[16,128,256]{2,0,1:T(8,128)S(1)} all-to-all(f32[16,128,256]{2,0,1:T(8,128)S(1)} %copy.25), channel_id=1, replica_groups=mesh['fsdp'=32,'tp'=4,'job'=2] {'fsdp'}, dimensions={1} | all-to-all | bytes 4194304 | tf_op jit(solution)/shard_map/all_to_all | solution.py:54
  205.5 0.2 broadcast_multiply_fusion
  205.8 0.2 copy.26
  206.0 1.4 copy-done.1
  207.4 0.4 bitcast_subtract_fusion
  207.8 2.7 %copy.28 = f32[512,4,256]{2,1,0:T(4,128)} copy(f32[512,4,256]{2,0,1:T(8,128)S(1)} %bitcast_subtract_fusion) | data formatting | bytes 4194304
  (7 shorter events, 0.6 us)
Async XLA Ops:
  3.6 62.3 %copy-start = (f32[512,4,256]{2,1,0:T(4,128)}, f32[512,4,256]{2,1,0:T(4,128)S(1)}, u32[]{:S(2)}) copy-start(f32[512,4,256]{2,1,0:T(4,128)S(1)} %multiply_add_fusion.5) | copy-start | bytes 6291460
  205.8 1.6 copy-start.1
where the time goes:
time: 211 us; the launch traced here: 210 us
  blocking collectives  175 us (83%)
  matrix products  23 us (11%)
  local copies, waits for them, and re-layouts  7.93 us (4%)
  other arithmetic  4.11 us (2%)
    all_to_all x1, blocking collectives, body(): lax.all_to_all(new_momentum, 'fsdp', split_axis=0, concat_axis=1, tiled=T...  61.9 us
    all_to_all x1, blocking collectives, body(): lax.all_to_all(iterate, 'fsdp', split_axis=1, concat_axis=0, tiled=True)  54.2 us
    all_to_all x2, blocking collectives, cut_exchange(): lax.all_to_all(share, axis, split_axis=0, concat_axis=0, tiled=True)  29.5 us
    all_to_all x1, blocking collectives, body(): whole = lax.all_to_all(moved, 'tp', split_axis=0, concat_axis=2, tiled=True)  29 us
    dot_general x5, matrix products, body(): jnp.einsum('mij,mjk->mik', mixed, iterate, precision=lax.Precision.HIGHEST)  10.7 us
    dot_general x5, matrix products, body(): jnp.einsum('mik,mjk->mij', iterate, iterate, precision=lax.Precision.HIGH...  10.5 us

commit v1 on v0

v1 whole, which is shorter than its diff:
```python
import jax
import jax.numpy as jnp
from jax import lax
from jax.sharding import PartitionSpec as P

ITERS = 5

hold_rate = 0.9
learn_rate = 0.8


def body(slopes_in, moments_in, weights_in):
    new_momentum = hold_rate * moments_in + slopes_in
    rows_axis = lax.axis_size("fsdp")
    cols_axis = lax.axis_size("tp")
    mats, rows, cols = new_momentum.shape
    own = mats // (rows_axis * cols_axis)
    moved = lax.all_to_all(
        new_momentum.reshape(rows_axis * cols_axis, own, rows, cols), ("fsdp", "tp"), 0, 0, tiled=True
    )
    iterate = moved.reshape(rows_axis, cols_axis, own, rows, cols).transpose(2, 0, 3, 1, 4)
    iterate = iterate.reshape(own, rows_axis * rows, cols_axis * cols)
    iterate = iterate * lax.rsqrt(jnp.sum(iterate * iterate, axis=(1, 2), keepdims=True) + 1e-06)
    for step in range(ITERS):
        gram = jnp.einsum("mik,mjk->mij", iterate, iterate, precision=lax.Precision.HIGHEST)
        mixed = -4.775 * gram + 2.0315 * jnp.einsum(
            "mij,mjk->mik", gram, gram, precision=lax.Precision.HIGHEST
        )
        iterate = 3.4445 * iterate + jnp.einsum(
            "mij,mjk->mik", mixed, iterate, precision=lax.Precision.HIGHEST
        )
    back = iterate.reshape(own, rows_axis, rows, cols_axis, cols).transpose(1, 3, 0, 2, 4)
    back = lax.all_to_all(
        back.reshape(rows_axis * cols_axis, own, rows, cols), ("fsdp", "tp"), 0, 0, tiled=True
    )
    new_weights = weights_in - learn_rate * back.reshape(mats, rows, cols)
    return (new_weights, new_momentum)


def solution(mesh):
    placed = P("job", "fsdp", "tp")
    return jax.shard_map(
        body, mesh=mesh, in_specs=(placed,) * 3, out_specs=(placed,) * 2, check_vma=False
    )
```

time: 211 us -> 168 us (0.80)
  the two profiles are of different devices: /device:TPU:16 before, /device:TPU:32 now
where the time goes in v1:
time: 168 us
  blocking collectives  127 us (76%)
  matrix products  23 us (14%)
  local copies, waits for them, and re-layouts  10.5 us (6%)
  other arithmetic  6.17 us (4%)
    all_to_all x1, blocking collectives, body(): lax.all_to_all(new_momentum.reshape(rows_axis * cols_axis, own, rows, col...  68.1 us
    all_to_all x1, blocking collectives, body(): lax.all_to_all(back.reshape(rows_axis * cols_axis, own, rows, cols), ('fs...  59 us
    dot_general x5, matrix products, body(): jnp.einsum('mij,mjk->mik', mixed, iterate, precision=lax.Precision.HIGHEST)  10.7 us
    dot_general x5, matrix products, body(): jnp.einsum('mik,mjk->mij', iterate, iterate, precision=lax.Precision.HIGH...  10.5 us
    reshape x2, local copies, waits for them, and re-layouts, body(): iterate.reshape(own, rows_axis, rows, cols_axis, cols)  4.27 us

profile of v1, /device:TPU:32, one launch (start us, length us, event | category | flops | bytes accessed | tf_op | source)
XLA Modules:
  0.0 167.6 jit_solution(11675005075830640674)
XLA Ops:
  0.6 2.9 %multiply_add_fusion.5 = f32[512,4,256]{2,1,0:T(4,128)S(1)} fusion(f32[512,4,256]{2,1,0:T(4,128)} %param.3, f32[512,4,256]{2,1,0:T(4,128)} %param.4), kind=kLoop, calls=%fused_computation.7 | loop fusion | flops 1048576 | bytes 6291456 | tf_op jit(solution)/shard_map/add | solution.py:13
  3.6 0.0 copy-start
  3.6 68.1 %all_to_all.10 = f32[128,4,4,256]{3,2,1,0:T(4,128)S(1)} all-to-all(f32[128,4,4,256]{3,2,1,0:T(4,128)S(1)} %bitcast.38), channel_id=1, replica_groups=mesh['fsdp'=32,'tp'=4,'job'=2] {'fsdp','tp'}, dimensions={0} | all-to-all | bytes 4194304 | tf_op jit(solution)/shard_map/all_to_all | solution.py:18
  71.7 0.0 copy-done
  71.7 0.6 multiply_reduce_fusion
  72.4 2.7 %copy.5 = f32[4,32,4,4,256]{4,3,2,1,0:T(4,128)} copy(f32[4,32,4,4,256]{4,2,0,3,1:T(4,128)S(1)} %bitcast.37) | data formatting | bytes 4194304 | tf_op jit(solution)/shard_map/transpose | solution.py:21
  75.0 2.5 %reshape.30 = f32[4,128,1024]{2,1,0:T(8,128)S(1)} reshape(f32[4,32,4,4,256]{4,3,2,1,0:T(4,128)} %copy.5) | data formatting | bytes 4194304 | tf_op jit(solution)/shard_map/reshape | solution.py:22
  77.6 2.3 %fusion.2 = f32[4,128,128]{2,1,0:T(8,128)S(1)} fusion(f32[4,128,1024]{2,1,0:T(8,128)S(1)} %reshape.30, f32[4]{0:T(128)S(1)} %add_rsqrt_fusion), kind=kOutput, calls=%fused_computation.10 | convolution fusion | flops 805830656 | bytes 2359312 | tf_op jit(solution)/shard_map/mik,mjk->mij/dot_general | solution.py:25
  79.8 0.4 fusion.10
  80.2 2.2 %multiply_add_fusion.4 = f32[4,128,1024]{2,1,0:T(8,128)S(1)} fusion(f32[4,128,1024]{2,1,0:T(8,128)S(1)} %reshape.30, f32[4,128,128]{2,1,0:T(8,128)S(1)} %fusion.10, f32[4]{0:T(128)S(1)} %add_rsqrt_fusion), kind=kOutput, calls=%fused_computation.5 | convolution fusion | flops 807403520 | bytes 4456464 | tf_op jit(solution)/shard_map/mij,mjk->mik/dot_general | solution.py:29
  82.4 2.0 %fusion.13 = f32[4,128,128]{2,1,0:T(8,128)S(1)} fusion(f32[4,128,1024]{2,1,0:T(8,128)S(1)} %multiply_add_fusion.4), kind=kOutput, calls=%fused_computation.26 | convolution fusion | flops 805306368 | bytes 2359296 | tf_op jit(solution)/shard_map/mik,mjk->mij/dot_general | solution.py:25
  84.4 0.4 fusion.9
  84.8 2.1 %multiply_add_fusion.3 = f32[4,128,1024]{2,1,0:T(8,128)S(1)} fusion(f32[4,128,1024]{2,1,0:T(8,128)S(1)} %multiply_add_fusion.4, f32[4,128,128]{2,1,0:T(8,128)S(1)} %fusion.9), kind=kOutput, calls=%fused_computation.4 | convolution fusion | flops 806354944 | bytes 4456448 | tf_op jit(solution)/shard_map/mij,mjk->mik/dot_general | solution.py:29
  86.9 2.0 %fusion.14 = f32[4,128,128]{2,1,0:T(8,128)S(1)} fusion(f32[4,128,1024]{2,1,0:T(8,128)S(1)} %multiply_add_fusion.3), kind=kOutput, calls=%fused_computation.27 | convolution fusion | flops 805306368 | bytes 2359296 | tf_op jit(solution)/shard_map/mik,mjk->mij/dot_general | solution.py:25
  89.0 0.4 fusion.8
  89.3 2.3 %multiply_add_fusion.2 = f32[4,128,1024]{2,1,0:T(8,128)S(1)} fusion(f32[4,128,1024]{2,1,0:T(8,128)S(1)} %multiply_add_fusion.3, f32[4,128,128]{2,1,0:T(8,128)S(1)} %fusion.8), kind=kOutput, calls=%fused_computation.3 | convolution fusion | flops 806354944 | bytes 4456448 | tf_op jit(solution)/shard_map/mij,mjk->mik/dot_general | solution.py:29
  91.7 2.1 %fusion.15 = f32[4,128,128]{2,1,0:T(8,128)S(1)} fusion(f32[4,128,1024]{2,1,0:T(8,128)S(1)} %multiply_add_fusion.2), kind=kOutput, calls=%fused_computation.28 | convolution fusion | flops 805306368 | bytes 2359296 | tf_op jit(solution)/shard_map/mik,mjk->mij/dot_general | solution.py:25
  93.7 0.4 fusion.7
  94.1 2.1 %multiply_add_fusion.1 = f32[4,128,1024]{2,1,0:T(8,128)S(1)} fusion(f32[4,128,1024]{2,1,0:T(8,128)S(1)} %multiply_add_fusion.2, f32[4,128,128]{2,1,0:T(8,128)S(1)} %fusion.7), kind=kOutput, calls=%fused_computation.2 | convolution fusion | flops 806354944 | bytes 4456448 | tf_op jit(solution)/shard_map/mij,mjk->mik/dot_general | solution.py:29
  96.2 2.0 %fusion.16 = f32[4,128,128]{2,1,0:T(8,128)S(1)} fusion(f32[4,128,1024]{2,1,0:T(8,128)S(1)} %multiply_add_fusion.1), kind=kOutput, calls=%fused_computation.29 | convolution fusion | flops 805306368 | bytes 2359296 | tf_op jit(solution)/shard_map/mik,mjk->mij/dot_general | solution.py:25
  98.2 0.4 fusion.6
  98.6 2.1 %multiply_add_fusion = f32[4,128,1024]{2,1,0:T(8,128)S(1)} fusion(f32[4,128,1024]{2,1,0:T(8,128)S(1)} %multiply_add_fusion.1, f32[4,128,128]{2,1,0:T(8,128)S(1)} %fusion.6), kind=kOutput, calls=%fused_computation.1 | convolution fusion | flops 806354944 | bytes 4456448 | tf_op jit(solution)/shard_map/mij,mjk->mik/dot_general | solution.py:29
  100.7 2.0 %reshape.31 = f32[4,32,4,4,256]{4,3,2,1,0:T(4,128)} reshape(f32[4,128,1024]{2,1,0:T(8,128)S(1)} %multiply_add_fusion) | data formatting | bytes 4194304 | tf_op jit(solution)/shard_map/reshape | solution.py:32
  102.7 2.3 %copy.6 = f32[4,32,4,4,256]{4,2,0,3,1:T(4,128)S(1)} copy(f32[4,32,4,4,256]{4,3,2,1,0:T(4,128)} %reshape.31) | data formatting | bytes 4194304 | tf_op jit(solution)/shard_map/reshape | solution.py:32
  105.0 59.0 %all_to_all.11 = f32[128,4,4,256]{3,2,1,0:T(4,128)S(1)} all-to-all(f32[128,4,4,256]{3,2,1,0:T(4,128)S(1)} %bitcast.39), channel_id=1, replica_groups=mesh['fsdp'=32,'tp'=4,'job'=2] {'fsdp','tp'}, dimensions={0} | all-to-all | bytes 4194304 | tf_op jit(solution)/shard_map/all_to_all | solution.py:33
  164.0 0.0 copy-start.1
  164.0 0.6 broadcast_multiply_fusion
  164.6 1.0 copy-done.1
  165.6 2.0 %bitcast_subtract_fusion = f32[512,4,256]{2,1,0:T(4,128)} fusion(f32[512,4,256]{2,1,0:T(4,128)S(1)} %copy-done.1, f32[128,4,4,256]{3,2,1,0:T(4,128)S(1)} %broadcast_multiply_fusion), kind=kLoop, calls=%fused_computation | loop fusion | flops 524288 | bytes 6291456 | tf_op jit(solution)/shard_map/sub | solution.py:36
  (1 shorter events, 0.0 us)
Async XLA Ops:
  3.6 68.2 %copy-start = (f32[512,4,256]{2,1,0:T(4,128)}, f32[512,4,256]{2,1,0:T(4,128)S(1)}, u32[]{:S(2)}) copy-start(f32[512,4,256]{2,1,0:T(4,128)S(1)} %multiply_add_fusion.5) | copy-start | bytes 6291460
  164.0 1.6 copy-start.1

commit v2 on v1

v2 whole, which is shorter than its diff:
```python
import jax
import jax.numpy as jnp
from jax import lax
from jax.experimental import pallas as pl
from jax.experimental.pallas import tpu as pltpu
from jax.sharding import PartitionSpec as P

ITERS = 5
WINDOWS = (2, 3)

hold_rate = 0.9
learn_rate = 0.8

ROWS_BY_ROWS = (((1,), (1,)), ((), ()))
ROWS_BY_COLS = (((1,), (0,)), ((), ()))


def product(left, right, dims=ROWS_BY_COLS):
    return lax.dot_general(
        left, right, dims, precision=lax.Precision.HIGHEST, preferred_element_type=jnp.float32
    )


def orthogonalize(stack):
    side = stack[0].shape[0]
    unit = lax.broadcasted_iota(jnp.int32, (side, side), 0) == lax.broadcasted_iota(
        jnp.int32, (side, side), 1
    )
    scaled_unit = 3.4445 * unit.astype(jnp.float32)
    stack = [x * lax.rsqrt(jnp.sum(x * x, keepdims=True) + 1e-06) for x in stack]
    assert sum(WINDOWS) == ITERS
    for window in WINDOWS:
        grams = [product(x, x, ROWS_BY_ROWS) for x in stack]
        total = None
        for step in range(window):
            mixed = [scaled_unit + (-4.775 * a + 2.0315 * product(a, a)) for a in grams]
            total = mixed if total is None else [product(m, t) for m, t in zip(mixed, total)]
            if step < window - 1:
                grams = [product(product(m, a), m) for m, a in zip(mixed, grams)]
        stack = [product(t, x) for t, x in zip(total, stack)]
    return stack


def kernel(moved, back, whole):
    groups, cuts, own, rows, cols = moved.shape

    def gather(pair, carry):
        for m in range(own):
            for x in range(cuts):
                columns = slice(x * cols, (x + 1) * cols)
                whole[m, pair, 0:rows, columns] = moved[2 * pair, x, m]
                whole[m, pair, rows : 2 * rows, columns] = moved[2 * pair + 1, x, m]
        return carry

    def scatter(pair, carry):
        for m in range(own):
            for x in range(cuts):
                columns = slice(x * cols, (x + 1) * cols)
                back[2 * pair, x, m] = whole[m, pair, 0:rows, columns]
                back[2 * pair + 1, x, m] = whole[m, pair, rows : 2 * rows, columns]
        return carry

    lax.fori_loop(0, groups // 2, gather, 0, unroll=2)
    stack = orthogonalize([whole[m].reshape(groups * rows, cuts * cols) for m in range(own)])
    for m in range(own):
        whole[m] = (learn_rate * stack[m]).reshape(groups // 2, 2 * rows, cuts * cols)
    lax.fori_loop(0, groups // 2, scatter, 0, unroll=2)


def steps_of(moved):
    groups, cuts, own, rows, cols = moved.shape
    return pl.pallas_call(
        kernel,
        out_shape=jax.ShapeDtypeStruct(moved.shape, moved.dtype),
        in_specs=[pl.BlockSpec(memory_space=pltpu.VMEM)],
        out_specs=pl.BlockSpec(memory_space=pltpu.VMEM),
        scratch_shapes=[pltpu.VMEM((own, groups // 2, 2 * rows, cuts * cols), jnp.float32)],
        compiler_params=pltpu.CompilerParams(vmem_limit_bytes=32 * 2**20),
        name="steps",
    )(moved)


def body(slopes_in, moments_in, weights_in):
    new_momentum = hold_rate * moments_in + slopes_in
    groups = lax.axis_size("fsdp")
    cuts = lax.axis_size("tp")
    mats, rows, cols = new_momentum.shape
    own = mats // (groups * cuts)
    moved = lax.all_to_all(
        new_momentum.reshape(groups * cuts, own, rows, cols), ("fsdp", "tp"), 0, 0, tiled=True
    )
    back = steps_of(moved.reshape(groups, cuts, own, rows, cols))
    back = lax.all_to_all(
        back.reshape(groups * cuts, own, rows, cols), ("fsdp", "tp"), 0, 0, tiled=True
    )
    new_weights = weights_in - back.reshape(mats, rows, cols)
    return (new_weights, new_momentum)


def solution(mesh):
    placed = P("job", "fsdp", "tp")
    return jax.shard_map(
        body, mesh=mesh, in_specs=(placed,) * 3, out_specs=(placed,) * 2, check_vma=False
    )
```

time: 168 us -> 144 us (0.86)
  matrix products: 23 us -> 0 us
  Pallas kernels: 0 us -> 11 us
  local copies, waits for them, and re-layouts: 10.5 us -> 0.01 us
    dot_general x15 -> x0, matrix products: 23 us -> none  [the longest x5 10.7 us: body(): jnp.einsum('mij,mjk->mik', mixed, iterate, precision=lax.Precision.HIGHEST)]
    pallas_call x0 -> x1, Pallas kernels: none -> 11 us  [steps_of(): pl.pallas_call(kernel, out_shape=jax.ShapeDtypeStruct(moved.shape, moved....]
    reshape x3 -> x0, local copies, waits for them, and re-layouts: 6.79 us -> none  [the longest x2 4.27 us: body(): iterate.reshape(own, rows_axis, rows, cols_axis, cols)]
    transpose x1 -> x0, local copies, waits for them, and re-layouts: 2.67 us -> none  [body(): moved.reshape(rows_axis, cols_axis, own, rows, cols)]
where the time goes in v2:
time: 144 us
  blocking collectives  127 us (88%)
  Pallas kernels  11 us (8%)
  other arithmetic  4.94 us (3%)
    all_to_all x1, blocking collectives, body(): lax.all_to_all(new_momentum.reshape(groups * cuts, own, rows, cols), ('fs...  68.1 us
    all_to_all x1, blocking collectives, body(): lax.all_to_all(back.reshape(groups * cuts, own, rows, cols), ('fsdp', 'tp...  59.2 us
    pallas_call x1, Pallas kernels, steps_of(): pl.pallas_call(kernel, out_shape=jax.ShapeDtypeStruct(moved.shape, moved....  11 us
    add x1, other arithmetic, body(): new_momentum = hold_rate * moments_in + slopes_in  2.94 us

profile of v2, /device:TPU:32, one launch (start us, length us, event | category | flops | bytes accessed | tf_op | source)
XLA Modules:
  0.0 143.9 jit_solution(2512833898872420986)
XLA Ops:
  0.6 2.9 %multiply_add_fusion = f32[512,4,256]{2,1,0:T(4,128)S(1)} fusion(f32[512,4,256]{2,1,0:T(4,128)} %param.3, f32[512,4,256]{2,1,0:T(4,128)} %param.4), kind=kLoop, calls=%fused_computation.1 | loop fusion | flops 1048576 | bytes 6291456 | tf_op jit(solution)/shard_map/add | solution.py:84
  3.6 0.0 copy-start
  3.6 68.1 %all_to_all.10 = f32[128,4,4,256]{3,2,1,0:T(4,128)S(1)} all-to-all(f32[128,4,4,256]{3,2,1,0:T(4,128)S(1)} %bitcast.7), channel_id=1, replica_groups=mesh['fsdp'=32,'tp'=4,'job'=2] {'fsdp','tp'}, dimensions={0} | all-to-all | bytes 4194304 | tf_op jit(solution)/shard_map/all_to_all | solution.py:89
  71.7 0.0 copy-done
  71.7 11.0 %steps.1 = f32[32,4,4,4,256]{4,3,2,1,0:T(4,128)S(1)} custom-call(f32[32,4,4,4,256]{4,3,2,1,0:T(4,128)S(1)} %bitcast.6), custom_call_target="tpu_custom_call" | custom-call | tf_op jit(solution)/shard_map/steps/pallas_call | solution.py:72
  82.7 0.0 copy-start.1
  82.7 59.2 %all_to_all.11 = f32[128,4,4,256]{3,2,1,0:T(4,128)S(1)} all-to-all(f32[128,4,4,256]{3,2,1,0:T(4,128)S(1)} %bitcast.5), channel_id=1, replica_groups=mesh['fsdp'=32,'tp'=4,'job'=2] {'fsdp','tp'}, dimensions={0} | all-to-all | bytes 4194304 | tf_op jit(solution)/shard_map/all_to_all | solution.py:93
  141.9 0.0 copy-done.1
  141.9 2.0 %bitcast_subtract_fusion = f32[512,4,256]{2,1,0:T(4,128)} fusion(f32[512,4,256]{2,1,0:T(4,128)S(1)} %copy-done.1, f32[128,4,4,256]{3,2,1,0:T(4,128)S(1)} %all_to_all.11), kind=kLoop, calls=%fused_computation | loop fusion | flops 524288 | bytes 6291456 | tf_op jit(solution)/shard_map/sub | solution.py:96
Async XLA Ops:
  3.6 68.2 %copy-start = (f32[512,4,256]{2,1,0:T(4,128)}, f32[512,4,256]{2,1,0:T(4,128)S(1)}, u32[]{:S(2)}) copy-start(f32[512,4,256]{2,1,0:T(4,128)S(1)} %multiply_add_fusion) | copy-start | bytes 6291460
  82.7 59.2 %copy-start.1 = (f32[512,4,256]{2,1,0:T(4,128)S(1)}, f32[512,4,256]{2,1,0:T(4,128)}, u32[]{:S(2)}) copy-start(f32[512,4,256]{2,1,0:T(4,128)} %param.5) | copy-start | bytes 6291460

commit v3 on v2

--- a/solution.py
+++ b/solution.py
@@ -11,14 +11,47 @@
 hold_rate = 0.9
 learn_rate = 0.8
 
+TURN_NS = 25000
+
 ROWS_BY_ROWS = (((1,), (1,)), ((), ()))
 ROWS_BY_COLS = (((1,), (0,)), ((), ()))
 
 
-def product(left, right, dims=ROWS_BY_COLS):
+def product(left, right):
     return lax.dot_general(
-        left, right, dims, precision=lax.Precision.HIGHEST, preferred_element_type=jnp.float32
+        left,
+        right,
+        ROWS_BY_COLS,
+        precision=lax.Precision.HIGHEST,
+        preferred_element_type=jnp.float32,
     )
+
+
+def split(x):
+    high = x.astype(jnp.bfloat16)
+    rest = x - high.astype(jnp.float32)
+    middle = rest.astype(jnp.bfloat16)
+    low = (rest - middle.astype(jnp.float32)).astype(jnp.bfloat16)
+    return high, middle, low
+
+
+def term(left, right, dims=ROWS_BY_COLS):
+    return lax.dot_general(left, right, dims, preferred_element_type=jnp.float32)
+
+
+def gram_of(x):
+    high, middle, low = split(x)
+    mixed = term(high, middle, ROWS_BY_ROWS) + term(high, low, ROWS_BY_ROWS)
+    small = mixed + mixed.T + term(middle, middle, ROWS_BY_ROWS)
+    return term(high, high, ROWS_BY_ROWS) + small
+
+
+def applied(left, right):
+    lh, lm, ll = split(left)
+    rh, rm, rl = split(right)
+    pair = term(jnp.concatenate((lh, lm), 1), jnp.concatenate((rm, rh), 0))
+    small = term(jnp.concatenate((lh, ll), 1), jnp.concatenate((rl, rh), 0)) + term(lm, rm)
+    return term(lh, rh) + (pair + small)
 
 
 def orthogonalize(stack):
@@ -30,14 +63,14 @@
     stack = [x * lax.rsqrt(jnp.sum(x * x, keepdims=True) + 1e-06) for x in stack]
     assert sum(WINDOWS) == ITERS
     for window in WINDOWS:
-        grams = [product(x, x, ROWS_BY_ROWS) for x in stack]
+        grams = [gram_of(x) for x in stack]
         total = None
         for step in range(window):
             mixed = [scaled_unit + (-4.775 * a + 2.0315 * product(a, a)) for a in grams]
             total = mixed if total is None else [product(m, t) for m, t in zip(mixed, total)]
             if step < window - 1:
                 grams = [product(product(m, a), m) for m, a in zip(mixed, grams)]
-        stack = [product(t, x) for t, x in zip(total, stack)]
+        stack = [applied(t, x) for t, x in zip(total, stack)]
     return stack
 
 
@@ -80,8 +113,55 @@
     )(moved)
 
 
+def momentum_kernel(slopes_hbm, moments_hbm, momentum, slopes, moments, arrived):
+    chunks = arrived.shape[1]
+    per = slopes.shape[0] // chunks
+    copies = []
+    for c in range(chunks):
+        part = pl.ds(c * per, per)
+        copies.append(
+            (
+                pltpu.make_async_copy(slopes_hbm.at[part], slopes.at[part], arrived.at[0, c]),
+                pltpu.make_async_copy(moments_hbm.at[part], moments.at[part], arrived.at[1, c]),
+            )
+        )
+        for copy in copies[-1]:
+            copy.start()
+    for c in range(chunks):
+        for copy in copies[c]:
+            copy.wait()
+
+        def some(i, carry):
+            part = pl.ds(c * per + i * 16, 16)
+            momentum[part] = hold_rate * moments[part] + slopes[part]
+            return carry
+
+        lax.fori_loop(0, per // 16, some, 0)
+
+    @pl.when(lax.axis_index("job") == 1)
+    def _():
+        pl.delay(TURN_NS)
+
+
+def momentum_of(slopes_in, moments_in):
+    hbm = [pltpu.with_memory_space_constraint(x, pltpu.HBM) for x in (slopes_in, moments_in)]
+    return pl.pallas_call(
+        momentum_kernel,
+        out_shape=jax.ShapeDtypeStruct(slopes_in.shape, slopes_in.dtype),
+        in_specs=[pl.BlockSpec(memory_space=pltpu.HBM)] * 2,
+        out_specs=pl.BlockSpec(memory_space=pltpu.VMEM),
+        scratch_shapes=[
+            pltpu.VMEM(slopes_in.shape, jnp.float32),
+            pltpu.VMEM(slopes_in.shape, jnp.float32),
+            pltpu.SemaphoreType.DMA((2, 4)),
+        ],
+        compiler_params=pltpu.CompilerParams(vmem_limit_bytes=16 * 2**20),
+        name="momentum",
+    )(*hbm)
+
+
 def body(slopes_in, moments_in, weights_in):
-    new_momentum = hold_rate * moments_in + slopes_in
+    new_momentum = momentum_of(slopes_in, moments_in)
     groups = lax.axis_size("fsdp")
     cuts = lax.axis_size("tp")
     mats, rows, cols = new_momentum.shape

time: 144 us -> 126 us (0.88)
  the two profiles are of different devices: /device:TPU:32 before, /device:TPU:1 now
where the time goes in v3:
time: 126 us; the launch traced here: 125 us
  blocking collectives  85 us (67%)
  Pallas kernels  37.7 us (30%)
  other arithmetic  1.99 us (2%)
    all_to_all x1, blocking collectives, body(): lax.all_to_all(new_momentum.reshape(groups * cuts, own, rows, cols), ('fs...  46.9 us
    all_to_all x1, blocking collectives, body(): lax.all_to_all(back.reshape(groups * cuts, own, rows, cols), ('fsdp', 'tp...  38 us
    pallas_call x1, Pallas kernels, momentum_of(): pl.pallas_call(momentum_kernel, out_shape=jax.ShapeDtypeStruct(slopes_in....  28.6 us
    pallas_call x1, Pallas kernels, steps_of(): pl.pallas_call(kernel, out_shape=jax.ShapeDtypeStruct(moved.shape, moved....  9.04 us

profile of v3, /device:TPU:1, one launch (start us, length us, event | category | flops | bytes accessed | tf_op | source)
XLA Modules:
  0.0 125.3 jit_solution(17179654934044028617)
XLA Ops:
  0.6 28.6 %momentum.1 = f32[512,4,256]{2,1,0:T(4,128)} custom-call(f32[512,4,256]{2,1,0:T(4,128)} %slopes_hbm.1, f32[512,4,256]{2,1,0:T(4,128)} %moments_hbm.1), custom_call_target="tpu_custom_call" | custom-call | tf_op jit(solution)/shard_map/momentum/pallas_call | solution.py:148
  29.3 46.9 %all_to_all.10 = f32[128,4,4,256]{3,2,1,0:T(4,128)S(1)} all-to-all(f32[128,4,4,256]{3,2,1,0:T(4,128)} %bitcast.7), channel_id=1, replica_groups=mesh['fsdp'=32,'tp'=4,'job'=2] {'fsdp','tp'}, dimensions={0} | all-to-all | bytes 4194304 | tf_op jit(solution)/shard_map/all_to_all | solution.py:169
  76.2 9.0 %steps.1 = f32[32,4,4,4,256]{4,3,2,1,0:T(4,128)S(1)} custom-call(f32[32,4,4,4,256]{4,3,2,1,0:T(4,128)S(1)} %bitcast.6), custom_call_target="tpu_custom_call" | custom-call | tf_op jit(solution)/shard_map/steps/pallas_call | solution.py:105
  85.3 0.0 copy-start
  85.3 38.0 %all_to_all.11 = f32[128,4,4,256]{3,2,1,0:T(4,128)S(1)} all-to-all(f32[128,4,4,256]{3,2,1,0:T(4,128)S(1)} %bitcast.5), channel_id=1, replica_groups=mesh['fsdp'=32,'tp'=4,'job'=2] {'fsdp','tp'}, dimensions={0} | all-to-all | bytes 4194304 | tf_op jit(solution)/shard_map/all_to_all | solution.py:173
  123.3 0.0 copy-done
  123.3 2.0 %bitcast_subtract_fusion = f32[512,4,256]{2,1,0:T(4,128)} fusion(f32[512,4,256]{2,1,0:T(4,128)S(1)} %copy-done, f32[128,4,4,256]{3,2,1,0:T(4,128)S(1)} %all_to_all.11), kind=kLoop, calls=%fused_computation | loop fusion | flops 524288 | bytes 6291456 | tf_op jit(solution)/shard_map/sub | solution.py:176
Async XLA Ops:
  85.3 38.1 %copy-start = (f32[512,4,256]{2,1,0:T(4,128)S(1)}, f32[512,4,256]{2,1,0:T(4,128)}, u32[]{:S(2)}) copy-start(f32[512,4,256]{2,1,0:T(4,128)} %param.5) | copy-start | bytes 6291460

commit v4 on v3

--- a/solution.py
+++ b/solution.py
@@ -12,6 +12,9 @@
 learn_rate = 0.8
 
 TURN_NS = 25000
+
+CHUNKS = 4
+BLOCK = 16
 
 ROWS_BY_ROWS = (((1,), (1,)), ((), ()))
 ROWS_BY_COLS = (((1,), (0,)), ((), ()))
@@ -113,34 +116,42 @@
     )(moved)
 
 
-def momentum_kernel(slopes_hbm, moments_hbm, momentum, slopes, moments, arrived):
+def momentum_kernel(slopes_hbm, moments_hbm, momentum_hbm, slopes, moments, arrived, stored):
     chunks = arrived.shape[1]
     per = slopes.shape[0] // chunks
-    copies = []
-    for c in range(chunks):
-        part = pl.ds(c * per, per)
-        copies.append(
-            (
-                pltpu.make_async_copy(slopes_hbm.at[part], slopes.at[part], arrived.at[0, c]),
-                pltpu.make_async_copy(moments_hbm.at[part], moments.at[part], arrived.at[1, c]),
-            )
+    parts = [pl.ds(c * per, per) for c in range(chunks)]
+    loads = [
+        (
+            pltpu.make_async_copy(slopes_hbm.at[part], slopes.at[part], arrived.at[0, c]),
+            pltpu.make_async_copy(moments_hbm.at[part], moments.at[part], arrived.at[1, c]),
         )
-        for copy in copies[-1]:
+        for c, part in enumerate(parts)
+    ]
+    stores = [
+        pltpu.make_async_copy(slopes.at[part], momentum_hbm.at[part], stored.at[c])
+        for c, part in enumerate(parts)
+    ]
+    for pair in loads:
+        for copy in pair:
             copy.start()
     for c in range(chunks):
-        for copy in copies[c]:
+        for copy in loads[c]:
             copy.wait()
 
         def some(i, carry):
-            part = pl.ds(c * per + i * 16, 16)
-            momentum[part] = hold_rate * moments[part] + slopes[part]
+            part = pl.ds(c * per + i * BLOCK, BLOCK)
+            slopes[part] = hold_rate * moments[part] + slopes[part]
             return carry
 
-        lax.fori_loop(0, per // 16, some, 0)
+        lax.fori_loop(0, per // BLOCK, some, 0)
+        stores[c].start()
 
     @pl.when(lax.axis_index("job") == 1)
     def _():
         pl.delay(TURN_NS)
+
+    for copy in stores:
+        copy.wait()
 
 
 def momentum_of(slopes_in, moments_in):
@@ -149,15 +160,50 @@
         momentum_kernel,
         out_shape=jax.ShapeDtypeStruct(slopes_in.shape, slopes_in.dtype),
         in_specs=[pl.BlockSpec(memory_space=pltpu.HBM)] * 2,
-        out_specs=pl.BlockSpec(memory_space=pltpu.VMEM),
+        out_specs=pl.BlockSpec(memory_space=pltpu.HBM),
         scratch_shapes=[
             pltpu.VMEM(slopes_in.shape, jnp.float32),
             pltpu.VMEM(slopes_in.shape, jnp.float32),
-            pltpu.SemaphoreType.DMA((2, 4)),
+            pltpu.SemaphoreType.DMA((2, CHUNKS)),
+            pltpu.SemaphoreType.DMA((CHUNKS,)),
         ],
         compiler_params=pltpu.CompilerParams(vmem_limit_bytes=16 * 2**20),
         name="momentum",
     )(*hbm)
+
+
+def weights_kernel(weights, back, new_hbm, new, stored):
+    chunks = stored.shape[0]
+    per = new.shape[0] // chunks
+    stores = []
+    for c in range(chunks):
+
+        def some(i, carry):
+            part = pl.ds(c * per + i * BLOCK, BLOCK)
+            new[part] = weights[part] - back[part]
+            return carry
+
+        lax.fori_loop(0, per // BLOCK, some, 0)
+        part = pl.ds(c * per, per)
+        stores.append(pltpu.make_async_copy(new.at[part], new_hbm.at[part], stored.at[c]))
+        stores[-1].start()
+    for copy in stores:
+        copy.wait()
+
+
+def weights_of(weights_in, back):
+    return pl.pallas_call(
+        weights_kernel,
+        out_shape=jax.ShapeDtypeStruct(weights_in.shape, weights_in.dtype),
+        in_specs=[pl.BlockSpec(memory_space=pltpu.VMEM)] * 2,
+        out_specs=pl.BlockSpec(memory_space=pltpu.HBM),
+        scratch_shapes=[
+            pltpu.VMEM(weights_in.shape, jnp.float32),
+            pltpu.SemaphoreType.DMA((CHUNKS,)),
+        ],
+        compiler_params=pltpu.CompilerParams(vmem_limit_bytes=16 * 2**20),
+        name="new_weights",
+    )(weights_in, back)
 
 
 def body(slopes_in, moments_in, weights_in):
@@ -173,7 +219,7 @@
     back = lax.all_to_all(
         back.reshape(groups * cuts, own, rows, cols), ("fsdp", "tp"), 0, 0, tiled=True
     )
-    new_weights = weights_in - back.reshape(mats, rows, cols)
+    new_weights = weights_of(weights_in, back.reshape(mats, rows, cols))
     return (new_weights, new_momentum)
 
 

time: 126 us -> 125 us (level)
  other arithmetic: 1.99 us -> 0 us
    sub x1 -> x0, other arithmetic: 1.99 us -> none  [body(): new_weights = weights_in - back.reshape(mats, rows, cols)]
    pallas_call x0 -> x1, Pallas kernels: none -> 1.42 us  [weights_of(): pl.pallas_call(weights_kernel, out_shape=jax.ShapeDtypeStruct(weights_in....]
    pallas_call x1, Pallas kernels: 28.6 us -> 27.4 us  [momentum_of(): pl.pallas_call(momentum_kernel, out_shape=jax.ShapeDtypeStruct(slopes_in....]
where the time goes in v4:
time: 125 us
  blocking collectives  86 us (69%)
  Pallas kernels  37.8 us (30%)
    all_to_all x1, blocking collectives, body(): lax.all_to_all(new_momentum.reshape(groups * cuts, own, rows, cols), ('fs...  47.1 us
    all_to_all x1, blocking collectives, body(): lax.all_to_all(back.reshape(groups * cuts, own, rows, cols), ('fsdp', 'tp...  38.9 us
    pallas_call x1, Pallas kernels, momentum_of(): pl.pallas_call(momentum_kernel, out_shape=jax.ShapeDtypeStruct(slopes_in....  27.4 us
    pallas_call x1, Pallas kernels, steps_of(): pl.pallas_call(kernel, out_shape=jax.ShapeDtypeStruct(moved.shape, moved....  9.04 us

profile of v4, /device:TPU:1, one launch (start us, length us, event | category | flops | bytes accessed | tf_op | source)
XLA Modules:
  0.0 124.5 jit_solution(14553017200183462683)
XLA Ops:
  0.6 27.4 %momentum.1 = f32[512,4,256]{2,1,0:T(4,128)} custom-call(f32[512,4,256]{2,1,0:T(4,128)} %slopes_hbm.1, f32[512,4,256]{2,1,0:T(4,128)} %moments_hbm.1), custom_call_target="tpu_custom_call" | custom-call | tf_op jit(solution)/shard_map/momentum/pallas_call | solution.py:159
  28.0 47.1 %all_to_all.10 = f32[128,4,4,256]{3,2,1,0:T(4,128)S(1)} all-to-all(f32[128,4,4,256]{3,2,1,0:T(4,128)} %bitcast.7), channel_id=1, replica_groups=mesh['fsdp'=32,'tp'=4,'job'=2] {'fsdp','tp'}, dimensions={0} | all-to-all | bytes 4194304 | tf_op jit(solution)/shard_map/all_to_all | solution.py:215
  75.1 9.0 %steps.1 = f32[32,4,4,4,256]{4,3,2,1,0:T(4,128)S(1)} custom-call(f32[32,4,4,4,256]{4,3,2,1,0:T(4,128)S(1)} %bitcast.6), custom_call_target="tpu_custom_call" | custom-call | tf_op jit(solution)/shard_map/steps/pallas_call | solution.py:108
  84.2 0.0 copy-start
  84.2 38.9 %all_to_all.11 = f32[128,4,4,256]{3,2,1,0:T(4,128)S(1)} all-to-all(f32[128,4,4,256]{3,2,1,0:T(4,128)S(1)} %bitcast.5), channel_id=1, replica_groups=mesh['fsdp'=32,'tp'=4,'job'=2] {'fsdp','tp'}, dimensions={0} | all-to-all | bytes 4194304 | tf_op jit(solution)/shard_map/all_to_all | solution.py:219
  123.1 0.0 copy-done
  123.1 1.4 %new_weights.1 = f32[512,4,256]{2,1,0:T(4,128)} custom-call(f32[512,4,256]{2,1,0:T(4,128)S(1)} %copy-done, f32[512,4,256]{2,1,0:T(4,128)S(1)} %bitcast.4), custom_call_target="tpu_custom_call" | custom-call | tf_op jit(solution)/shard_map/new_weights/pallas_call | solution.py:195
Async XLA Ops:
  84.2 38.9 %copy-start = (f32[512,4,256]{2,1,0:T(4,128)S(1)}, f32[512,4,256]{2,1,0:T(4,128)}, u32[]{:S(2)}) copy-start(f32[512,4,256]{2,1,0:T(4,128)} %weights.1) | copy-start | bytes 6291460

commit v5 on v4

--- a/solution.py
+++ b/solution.py
@@ -11,7 +11,7 @@
 hold_rate = 0.9
 learn_rate = 0.8
 
-TURN_NS = 25000
+TURN_NS = 24500
 
 CHUNKS = 4
 BLOCK = 16
@@ -77,8 +77,10 @@
     return stack
 
 
-def kernel(moved, back, whole):
+def kernel(moved, momentum, back, momentum_hbm, whole, stored):
     groups, cuts, own, rows, cols = moved.shape
+    store = pltpu.make_async_copy(momentum, momentum_hbm, stored)
+    store.start()
 
     def gather(pair, carry):
         for m in range(own):
@@ -101,22 +103,32 @@
     for m in range(own):
         whole[m] = (learn_rate * stack[m]).reshape(groups // 2, 2 * rows, cuts * cols)
     lax.fori_loop(0, groups // 2, scatter, 0, unroll=2)
-
-
-def steps_of(moved):
+    store.wait()
+
+
+def steps_of(moved, momentum):
     groups, cuts, own, rows, cols = moved.shape
     return pl.pallas_call(
         kernel,
-        out_shape=jax.ShapeDtypeStruct(moved.shape, moved.dtype),
-        in_specs=[pl.BlockSpec(memory_space=pltpu.VMEM)],
-        out_specs=pl.BlockSpec(memory_space=pltpu.VMEM),
-        scratch_shapes=[pltpu.VMEM((own, groups // 2, 2 * rows, cuts * cols), jnp.float32)],
+        out_shape=(
+            jax.ShapeDtypeStruct(moved.shape, moved.dtype),
+            jax.ShapeDtypeStruct(momentum.shape, momentum.dtype),
+        ),
+        in_specs=[pl.BlockSpec(memory_space=pltpu.VMEM)] * 2,
+        out_specs=(
+            pl.BlockSpec(memory_space=pltpu.VMEM),
+            pl.BlockSpec(memory_space=pltpu.HBM),
+        ),
+        scratch_shapes=[
+            pltpu.VMEM((own, groups // 2, 2 * rows, cuts * cols), jnp.float32),
+            pltpu.SemaphoreType.DMA(()),
+        ],
         compiler_params=pltpu.CompilerParams(vmem_limit_bytes=32 * 2**20),
         name="steps",
-    )(moved)
-
-
-def momentum_kernel(slopes_hbm, moments_hbm, momentum_hbm, slopes, moments, arrived, stored):
+    )(moved, momentum)
+
+
+def momentum_kernel(slopes_hbm, moments_hbm, momentum, slopes, moments, arrived):
     chunks = arrived.shape[1]
     per = slopes.shape[0] // chunks
     parts = [pl.ds(c * per, per) for c in range(chunks)]
@@ -127,10 +139,6 @@
         )
         for c, part in enumerate(parts)
     ]
-    stores = [
-        pltpu.make_async_copy(slopes.at[part], momentum_hbm.at[part], stored.at[c])
-        for c, part in enumerate(parts)
-    ]
     for pair in loads:
         for copy in pair:
             copy.start()
@@ -140,32 +148,27 @@
 
         def some(i, carry):
             part = pl.ds(c * per + i * BLOCK, BLOCK)
-            slopes[part] = hold_rate * moments[part] + slopes[part]
+            momentum[part] = hold_rate * moments[part] + slopes[part]
             return carry
 
         lax.fori_loop(0, per // BLOCK, some, 0)
-        stores[c].start()
 
     @pl.when(lax.axis_index("job") == 1)
     def _():
         pl.delay(TURN_NS)
-
-    for copy in stores:
-        copy.wait()
 
 
 def momentum_of(slopes_in, moments_in):
     hbm = [pltpu.with_memory_space_constraint(x, pltpu.HBM) for x in (slopes_in, moments_in)]
     return pl.pallas_call(
         momentum_kernel,
-        out_shape=jax.ShapeDtypeStruct(slopes_in.shape, slopes_in.dtype),
+        out_shape=pltpu.VMEM(slopes_in.shape, slopes_in.dtype),
         in_specs=[pl.BlockSpec(memory_space=pltpu.HBM)] * 2,
-        out_specs=pl.BlockSpec(memory_space=pltpu.HBM),
+        out_specs=pl.BlockSpec(memory_space=pltpu.VMEM),
         scratch_shapes=[
             pltpu.VMEM(slopes_in.shape, jnp.float32),
             pltpu.VMEM(slopes_in.shape, jnp.float32),
             pltpu.SemaphoreType.DMA((2, CHUNKS)),
-            pltpu.SemaphoreType.DMA((CHUNKS,)),
         ],
         compiler_params=pltpu.CompilerParams(vmem_limit_bytes=16 * 2**20),
         name="momentum",
@@ -207,15 +210,15 @@
 
 
 def body(slopes_in, moments_in, weights_in):
-    new_momentum = momentum_of(slopes_in, moments_in)
+    momentum = momentum_of(slopes_in, moments_in)
     groups = lax.axis_size("fsdp")
     cuts = lax.axis_size("tp")
-    mats, rows, cols = new_momentum.shape
+    mats, rows, cols = momentum.shape
     own = mats // (groups * cuts)
     moved = lax.all_to_all(
-        new_momentum.reshape(groups * cuts, own, rows, cols), ("fsdp", "tp"), 0, 0, tiled=True
-    )
-    back = steps_of(moved.reshape(groups, cuts, own, rows, cols))
+        momentum.reshape(groups * cuts, own, rows, cols), ("fsdp", "tp"), 0, 0, tiled=True
+    )
+    back, new_momentum = steps_of(moved.reshape(groups, cuts, own, rows, cols), momentum)
     back = lax.all_to_all(
         back.reshape(groups * cuts, own, rows, cols), ("fsdp", "tp"), 0, 0, tiled=True
     )

time: 125 us -> 123 us (0.984)
  no operation moved by 1% of the time
where the time goes in v5:
time: 123 us
  blocking collectives  85.4 us (69%)
  Pallas kernels  37.3 us (30%)
    all_to_all x1, blocking collectives, body(): lax.all_to_all(momentum.reshape(groups * cuts, own, rows, cols), ('fsdp',...  46.7 us
    all_to_all x1, blocking collectives, body(): lax.all_to_all(back.reshape(groups * cuts, own, rows, cols), ('fsdp', 'tp...  38.6 us
    pallas_call x1, Pallas kernels, momentum_of(): pl.pallas_call(momentum_kernel, out_shape=pltpu.VMEM(slopes_in.shape, slo...  26.8 us
    pallas_call x1, Pallas kernels, steps_of(): pl.pallas_call(kernel, out_shape=(jax.ShapeDtypeStruct(moved.shape, moved...  9.04 us

profile of v5, /device:TPU:1, one launch (start us, length us, event | category | flops | bytes accessed | tf_op | source)
XLA Modules:
  0.0 123.3 jit_solution(15634769307361402799)
XLA Ops:
  0.6 26.8 %momentum.1 = f32[512,4,256]{2,1,0:T(4,128)S(1)} custom-call(f32[512,4,256]{2,1,0:T(4,128)} %slopes_hbm.1, f32[512,4,256]{2,1,0:T(4,128)} %moments_hbm.1), custom_call_target="tpu_custom_call" | custom-call | tf_op jit(solution)/shard_map/momentum/pallas_call | solution.py:163
  27.4 46.7 %all_to_all.10 = f32[128,4,4,256]{3,2,1,0:T(4,128)S(1)} all-to-all(f32[128,4,4,256]{3,2,1,0:T(4,128)S(1)} %bitcast.4), channel_id=1, replica_groups=mesh['fsdp'=32,'tp'=4,'job'=2] {'fsdp','tp'}, dimensions={0} | all-to-all | bytes 4194304 | tf_op jit(solution)/shard_map/all_to_all | solution.py:218
  74.2 9.0 %steps.1 = (f32[32,4,4,4,256]{4,3,2,1,0:T(4,128)S(1)}, f32[512,4,256]{2,1,0:T(4,128)}) custom-call(f32[32,4,4,4,256]{4,3,2,1,0:T(4,128)S(1)} %bitcast.6, f32[512,4,256]{2,1,0:T(4,128)S(1)} %momentum.1), custom_call_target="tpu_custom_call" | custom-call | tf_op jit(solution)/shard_map/steps/pallas_call | solution.py:111
  83.2 0.0 copy-start
  83.2 38.6 %all_to_all.11 = f32[128,4,4,256]{3,2,1,0:T(4,128)S(1)} all-to-all(f32[128,4,4,256]{3,2,1,0:T(4,128)S(1)} %bitcast.7), channel_id=1, replica_groups=mesh['fsdp'=32,'tp'=4,'job'=2] {'fsdp','tp'}, dimensions={0} | all-to-all | bytes 4194304 | tf_op jit(solution)/shard_map/all_to_all | solution.py:222
  121.9 0.0 copy-done
  121.9 1.4 %new_weights.1 = f32[512,4,256]{2,1,0:T(4,128)} custom-call(f32[512,4,256]{2,1,0:T(4,128)S(1)} %copy-done, f32[512,4,256]{2,1,0:T(4,128)S(1)} %bitcast.5), custom_call_target="tpu_custom_call" | custom-call | tf_op jit(solution)/shard_map/new_weights/pallas_call | solution.py:198
Async XLA Ops:
  83.2 38.7 %copy-start = (f32[512,4,256]{2,1,0:T(4,128)S(1)}, f32[512,4,256]{2,1,0:T(4,128)}, u32[]{:S(2)}) copy-start(f32[512,4,256]{2,1,0:T(4,128)} %weights.1) | copy-start | bytes 6291460

commit v6 on v5

--- a/solution.py
+++ b/solution.py
@@ -62,17 +62,25 @@
     unit = lax.broadcasted_iota(jnp.int32, (side, side), 0) == lax.broadcasted_iota(
         jnp.int32, (side, side), 1
     )
-    scaled_unit = 3.4445 * unit.astype(jnp.float32)
-    stack = [x * lax.rsqrt(jnp.sum(x * x, keepdims=True) + 1e-06) for x in stack]
+    unit = unit.astype(jnp.float32)
+    scaled_unit = 3.4445 * unit
+    scales = None
     assert sum(WINDOWS) == ITERS
     for window in WINDOWS:
         grams = [gram_of(x) for x in stack]
+        if scales is None:
+            scales = [lax.rsqrt(jnp.sum(a * unit, keepdims=True) + 1e-06) for a in grams]
+            grams = [(r * r) * a for r, a in zip(scales, grams)]
+            factors = scales
+        else:
+            factors = [None] * len(stack)
         total = None
         for step in range(window):
             mixed = [scaled_unit + (-4.775 * a + 2.0315 * product(a, a)) for a in grams]
             total = mixed if total is None else [product(m, t) for m, t in zip(mixed, total)]
             if step < window - 1:
                 grams = [product(product(m, a), m) for m, a in zip(mixed, grams)]
+        total = [t if f is None else f * t for f, t in zip(factors, total)]
         stack = [applied(t, x) for t, x in zip(total, stack)]
     return stack
 

time: 123 us -> 123 us (level)
  no operation moved by 1% of the time
where the time goes in v6:
time: 123 us
  blocking collectives  85.3 us (69%)
  Pallas kernels  36.7 us (30%)
    all_to_all x1, blocking collectives, body(): lax.all_to_all(momentum.reshape(groups * cuts, own, rows, cols), ('fsdp',...  46.8 us
    all_to_all x1, blocking collectives, body(): lax.all_to_all(back.reshape(groups * cuts, own, rows, cols), ('fsdp', 'tp...  38.6 us
    pallas_call x1, Pallas kernels, momentum_of(): pl.pallas_call(momentum_kernel, out_shape=pltpu.VMEM(slopes_in.shape, slo...  26.8 us
    pallas_call x1, Pallas kernels, steps_of(): pl.pallas_call(kernel, out_shape=(jax.ShapeDtypeStruct(moved.shape, moved...  8.49 us

profile of v6, /device:TPU:1, one launch (start us, length us, event | category | flops | bytes accessed | tf_op | source)
XLA Modules:
  0.0 122.7 jit_solution(2870118218726120353)
XLA Ops:
  0.6 26.8 %momentum.1 = f32[512,4,256]{2,1,0:T(4,128)S(1)} custom-call(f32[512,4,256]{2,1,0:T(4,128)} %slopes_hbm.1, f32[512,4,256]{2,1,0:T(4,128)} %moments_hbm.1), custom_call_target="tpu_custom_call" | custom-call | tf_op jit(solution)/shard_map/momentum/pallas_call | solution.py:171
  27.4 46.8 %all_to_all.10 = f32[128,4,4,256]{3,2,1,0:T(4,128)S(1)} all-to-all(f32[128,4,4,256]{3,2,1,0:T(4,128)S(1)} %bitcast.4), channel_id=1, replica_groups=mesh['fsdp'=32,'tp'=4,'job'=2] {'fsdp','tp'}, dimensions={0} | all-to-all | bytes 4194304 | tf_op jit(solution)/shard_map/all_to_all | solution.py:226
  74.2 8.5 %steps.1 = (f32[32,4,4,4,256]{4,3,2,1,0:T(4,128)S(1)}, f32[512,4,256]{2,1,0:T(4,128)}) custom-call(f32[32,4,4,4,256]{4,3,2,1,0:T(4,128)S(1)} %bitcast.6, f32[512,4,256]{2,1,0:T(4,128)S(1)} %momentum.1), custom_call_target="tpu_custom_call" | custom-call | tf_op jit(solution)/shard_map/steps/pallas_call | solution.py:119
  82.7 0.0 copy-start
  82.7 38.6 %all_to_all.11 = f32[128,4,4,256]{3,2,1,0:T(4,128)S(1)} all-to-all(f32[128,4,4,256]{3,2,1,0:T(4,128)S(1)} %bitcast.7), channel_id=1, replica_groups=mesh['fsdp'=32,'tp'=4,'job'=2] {'fsdp','tp'}, dimensions={0} | all-to-all | bytes 4194304 | tf_op jit(solution)/shard_map/all_to_all | solution.py:230
  121.3 0.0 copy-done
  121.3 1.4 %new_weights.1 = f32[512,4,256]{2,1,0:T(4,128)} custom-call(f32[512,4,256]{2,1,0:T(4,128)S(1)} %copy-done, f32[512,4,256]{2,1,0:T(4,128)S(1)} %bitcast.5), custom_call_target="tpu_custom_call" | custom-call | tf_op jit(solution)/shard_map/new_weights/pallas_call | solution.py:206
Async XLA Ops:
  82.7 38.6 %copy-start = (f32[512,4,256]{2,1,0:T(4,128)S(1)}, f32[512,4,256]{2,1,0:T(4,128)}, u32[]{:S(2)}) copy-start(f32[512,4,256]{2,1,0:T(4,128)} %weights.1) | copy-start | bytes 6291460
